TPU v7x, 32 devices: a whole 2x2x4 slice. The times are simulated.
32 devices in a mesh: pipe: 4 (over x, core), exp: 4 (over z), pair: 2 (over y).
Axes of the slice: x: 2, y: 2, z: 4, core: 2. Of those that a mesh axis runs over, the one named last changes fastest.
Arguments:
- hidden_in: bfloat16 [4, 256, 2048], P(None, ('exp', 'pair')), may hold values from -6 to 6
- routes: int32 [4, 4, 256, 8], P('pipe', None, ('exp', 'pair')), may hold values from 0 to 15, all different within a row; in each aligned block of 32 rows (0 to 31, 32 to 63, ..., all dimensions but the last counted through in order) at most 24 rows name the same one
- gate_probs: float32 [4, 4, 256, 8], P('pipe', None, ('exp', 'pair')), may hold values from 0.02 to 1
- norm_gain: float32 [4, 2048], P('pipe'), may hold values from 0.1 to 1.9
- w_gate: bfloat16 [4, 16, 2048, 768], P('pipe', ('exp', 'pair')), may hold values from -0.125 to 0.125
- w_up: bfloat16 [4, 16, 2048, 768], P('pipe', ('exp', 'pair')), may hold values from -0.125 to 0.125
- w_down: bfloat16 [4, 16, 768, 2048], P('pipe', ('exp', 'pair')), may hold values from -0.21875 to 0.21875
Outputs:
- layer_outputs: bfloat16 [4, 4, 256, 2048], P('pipe', None, ('exp', 'pair'))
Inputs may be any that keep to these rules, and one draw needn't show every extreme that they name: `routes`: within each layer and micro-batch, the 32 tokens of one device (aligned blocks) name no expert more than 24 times in all, and each token names 8 different experts.
All inputs are finite; a program needn't handle non-finite values.
Results may differ from a plain program's by a relative error of at most 0.01.
Values may be sent and summed in bfloat16 or wider, within the bound.
A program may use at most 64 MiB of HBM per device.

v0:
```python
import functools

import jax
import jax.numpy as jnp
from jax import lax
from jax.experimental import pallas as pl
from jax.experimental.pallas import tpu as pltpu
from jax.sharding import PartitionSpec as P

EPS = 1e-06
MESH = pl.DeviceIdType.MESH
F32 = jnp.float32
BF16 = jnp.bfloat16
PIECES = 2
VMEM_LIMIT = 63 * 1024 * 1024


def divisor_tile(size, most):
    tile = most
    while size % tile:
        tile //= 2
    return tile


def relay_kernel(
    stages,
    zs,
    ys,
    pieces,
    hidden_ref,
    routes_ref,
    probs_ref,
    gain_ref,
    wgate_ref,
    wup_ref,
    wdown_ref,
    out_ref,
    wg,
    wu,
    wd,
    hbuf,
    tokens,
    share,
    hid,
    part,
    fromy,
    zsend,
    fromz,
    obuf,
    w_sem,
    h_sem,
    hs_sem,
    o_sem,
    s_sem,
    sr_sem,
    a_sem,
    ar_sem,
    y_sem,
    yr_sem,
    z_sem,
    zr_sem,
):
    micro, rows, width = hbuf.shape
    locals_, _, ff = wg.shape
    lanes = share.shape[3]
    groups = zs * ys
    experts = groups * locals_
    stage = lax.axis_index("pipe")
    z = lax.axis_index("exp")
    y = lax.axis_index("pair")
    me = z * ys + y
    slot = y * zs + z
    upper_half = lax.div(2 * z, zs)
    turn = 1 - 2 * upper_half

    def along(k):
        return lax.rem(z + turn * k + zs, zs)

    def peer(dz, dy):
        return lax.rem(z + dz, zs), lax.rem(y + dy, ys)

    others = [(dz, dy) for dy in range(ys) for dz in range(zs) if dz or dy]

    loads = []
    for j in range(locals_):
        loads.append(
            (
                pltpu.make_async_copy(wgate_ref.at[0, j], wg.at[j], w_sem.at[3 * j]),
                pltpu.make_async_copy(wup_ref.at[0, j], wu.at[j], w_sem.at[3 * j + 1]),
                pltpu.make_async_copy(
                    wdown_ref.at[0, j], wd.at[pl.ds(j * ff, ff)], w_sem.at[3 * j + 2]
                ),
            )
        )

    def from_input(m):
        return pltpu.make_async_copy(hidden_ref.at[m], hbuf.at[m], h_sem.at[m])

    @pl.when(stage == 0)
    def _():
        for m in range(micro):
            from_input(m).start()

    for j in range(locals_):
        loads[j][0].start()
        loads[j][1].start()
    for j in range(locals_):
        loads[j][2].start()

    barrier = pltpu.get_barrier_semaphore()
    for dz, dy in others:
        pz, py = peer(dz, dy)
        pl.semaphore_signal(barrier, inc=1, device_id={"exp": pz, "pair": py}, device_id_type=MESH)

    @pl.when(stage > 0)
    def _():
        pl.semaphore_signal(barrier, inc=1, device_id={"pipe": stage - 1}, device_id_type=MESH)

    @pl.when(stage < stages - 1)
    def _():
        pl.semaphore_signal(barrier, inc=1, device_id={"pipe": stage + 1}, device_id_type=MESH)

    lane = lax.broadcasted_iota(jnp.int32, (rows, lanes), 1)
    for m in range(micro):
        probs = probs_ref[0, m]
        normal = probs / jnp.sum(probs, axis=-1, keepdims=True)
        chosen = routes_ref[0, m]
        total = jnp.zeros((rows, lanes), F32)
        for k in range(chosen.shape[1]):
            named = chosen[:, k : k + 1]
            hit = jnp.logical_or(lane == named, lane == named + experts)
            total = total + jnp.where(hit, normal[:, k : k + 1], 0.0)
        high = total.astype(BF16)
        low = (total - high.astype(F32)).astype(BF16)
        share[slot, m] = jnp.where(lane < experts, high, low)

    linked = (stage > 0).astype(jnp.int32) + (stage < stages - 1).astype(jnp.int32)
    pl.semaphore_wait(barrier, len(others) + linked)

    def share_copy(at, to_z, to_y):
        return pltpu.make_async_remote_copy(
            src_ref=share.at[at],
            dst_ref=share.at[at],
            send_sem=s_sem.at[to_y * zs + to_z],
            recv_sem=sr_sem.at[at],
            device_id={"exp": to_z, "pair": to_y},
            device_id_type=MESH,
        )

    def share_send():
        for dz, dy in others:
            pz, py = peer(dz, dy)
            share_copy(slot, pz, py).start()

    def share_wait():
        for dz, dy in others:
            pz, py = peer(dz, dy)
            share_copy(py * zs + pz, pz, py).wait_recv()

    def token_copy(m, at, tag, to_z, to_y):
        block = tokens.at[m, pl.ds(pl.multiple_of(at * rows, rows), rows)]
        return pltpu.make_async_remote_copy(
            src_ref=block,
            dst_ref=block,
            send_sem=a_sem.at[m, tag],
            recv_sem=ar_sem.at[m, at],
            device_id={"exp": to_z, "pair": to_y},
            device_id_type=MESH,
        )

    def y_copy(m, dy, tz):
        py = lax.rem(y + dy, ys)
        return pltpu.make_async_remote_copy(
            src_ref=part.at[m, pl.ds(pl.multiple_of((py * zs + tz) * rows, rows), rows)],
            dst_ref=fromy.at[m, dy - 1, tz],
            send_sem=y_sem.at[m, dy - 1, tz],
            recv_sem=yr_sem.at[m, dy - 1, tz],
            device_id={"pair": py},
            device_id_type=MESH,
        )

    def z_copy(m, k, source):
        return pltpu.make_async_remote_copy(
            src_ref=zsend.at[m, k],
            dst_ref=fromz.at[m, source],
            send_sem=z_sem.at[m, k - 1],
            recv_sem=zr_sem.at[m, source],
            device_id={"exp": along(k)},
            device_id_type=MESH,
        )

    def hand_copy(m):
        return pltpu.make_async_remote_copy(
            src_ref=obuf.at[m],
            dst_ref=hbuf.at[m],
            send_sem=hs_sem.at[m],
            recv_sem=h_sem.at[m],
            device_id={"pipe": stage + 1},
            device_id_type=MESH,
        )

    def out_copy(m):
        return pltpu.make_async_copy(obuf.at[m], out_ref.at[0, m], o_sem.at[m])

    def announce(m):
        from_input(m).wait()
        state = hbuf[m].astype(F32)
        scale = lax.rsqrt(jnp.mean(state * state, axis=-1, keepdims=True) + EPS)
        tokens[m, pl.ds(pl.multiple_of(slot * rows, rows), rows)] = (
            state * scale * gain_ref[...]
        ).astype(BF16)
        for k in range(zs - 1, 0, -1):
            token_copy(m, slot, k - 1, along(k), y).start()
        for dy in range(1, ys):
            token_copy(m, slot, (zs - 1) + dy - 1, z, lax.rem(y + dy, ys)).start()

    nz = zs - 1

    def forward_tag(dz, dy):
        return nz + (ys - 1) + (dz - 1) * (ys - 1) + dy - 1

    def gather_z(m):
        for dz in range(1, zs):
            pz = along(dz)
            at = y * zs + pz
            token_copy(m, at, dz - 1, pz, y).wait_recv()
            for dy in range(1, ys):
                token_copy(m, at, forward_tag(dz, dy), z, lax.rem(y + dy, ys)).start()

    def gather_y(m, dy):
        py = lax.rem(y + dy, ys)
        for dz in range(zs):
            pz = lax.rem(z + dz, zs)
            token_copy(m, py * zs + pz, 0, z, py).wait_recv()

    ftile = divisor_tile(ff, 256)
    ntile = divisor_tile(width, 512)
    count = groups * rows

    def span(dy):
        return 0, pl.ds(0, count)

    def upper(m, dy):
        at, block = span(dy)
        wide = lax.broadcasted_iota(jnp.int32, (count, lanes), 1)
        shares = share[:, m].reshape(count, lanes).astype(F32)
        for j in range(locals_):
            expert = me * locals_ + j
            mine = jnp.logical_or(wide == expert, wide == expert + experts)
            column = jnp.sum(jnp.where(mine, shares, 0.0), axis=-1, keepdims=True)
            if dy == 0:

                @pl.when(m == 0)
                def _():
                    loads[j][0].wait()
                    loads[j][1].wait()

            for c in range(0, ff, ftile):
                held = tokens[m, block]
                gate = jnp.dot(held, wg[j, :, c : c + ftile], preferred_element_type=F32)
                upward = jnp.dot(held, wu[j, :, c : c + ftile], preferred_element_type=F32)
                hid[block, j * ff + c : j * ff + c + ftile] = (
                    jax.nn.silu(gate) * upward * column
                ).astype(BF16)

    def lower(m, dy):
        _, block = span(dy)
        for c in range(0, width, ntile):
            part[m, block, c : c + ntile] = jnp.dot(
                hid[block], wd[:, c : c + ntile], preferred_element_type=F32
            ).astype(BF16)

    def down_wait(m):
        @pl.when(m == 0)
        def _():
            for j in range(locals_):
                loads[j][2].wait()

    def own_part(m, pz):
        at = pl.multiple_of((y * zs + pz) * rows, rows)
        return part[m, pl.ds(at, rows)].astype(F32)

    def send_y(m, dy):
        for k in range(zs - 1, -1, -1):
            y_copy(m, dy, along(k)).start()

    def scatter(m):
        for k in range(zs - 1, 0, -1):
            pz = along(k)
            total = own_part(m, pz)
            for dy in range(1, ys):
                y_copy(m, dy, pz).wait_recv()
                total = total + fromy[m, dy - 1, pz].astype(F32)
            zsend[m, k] = total.astype(BF16)
            z_copy(m, k, z).start()

    def finish(m):
        total = hbuf[m].astype(F32) + own_part(m, z)
        for dy in range(1, ys):
            y_copy(m, dy, z).wait_recv()
            total = total + fromy[m, dy - 1, z].astype(F32)
        for k in range(1, zs):
            z_copy(m, k, along(k)).wait_recv()
            total = total + fromz[m, along(k)].astype(F32)
        obuf[m] = total.astype(BF16)

        @pl.when(stage < stages - 1)
        def _():
            hand_copy(m).start()

        out_copy(m).start()

    for i in range(pieces):
        announce(i)
    share_send()

    @pl.when(stage == 0)
    def _():
        for i in range(pieces):
            gather_z(i)

    @pl.loop(0, micro // pieces)
    def _(batch):
        m = batch * pieces
        following = m + pieces < micro
        first = jnp.logical_and(stage == 0, following)
        later = jnp.logical_and(stage > 0, following)

        @pl.when(stage > 0)
        def _():
            for i in range(pieces):
                gather_z(m + i)

        @pl.when(first)
        def _():
            for i in range(pieces):
                announce(m + pieces + i)

        @pl.when(m == 0)
        def _():
            share_wait()

        for i in range(pieces):
            for dy in range(1, ys):
                gather_y(m + i, dy)
            upper(m + i, 0)
            if i == 0:
                down_wait(m)
            lower(m + i, 0)
            for dy in range(1, ys):
                send_y(m + i, dy)

        @pl.when(first)
        def _():
            for i in range(pieces):
                gather_z(m + pieces + i)

        for i in range(pieces):
            scatter(m + i)
        for i in range(pieces):
            finish(m + i)

        @pl.when(later)
        def _():
            for i in range(pieces):
                announce(m + pieces + i)

    for dz, dy in others:
        pz, py = peer(dz, dy)
        share_copy(slot, pz, py).wait_send()

    @pl.loop(0, micro)
    def _(m):
        for tag in range(groups - 1):
            token_copy(m, slot, tag, z, y).wait_send()
        for dy in range(1, ys):
            for tz in range(zs):
                y_copy(m, dy, tz).wait_send()
        for dz in range(1, zs):
            z_copy(m, dz, z).wait_send()

        @pl.when(stage < stages - 1)
        def _():
            hand_copy(m).wait_send()

        out_copy(m).wait()


def relayed(hidden_in, routes, gate_probs, norm_gain, w_gate, w_up, w_down):
    batches, whole_rows, _ = hidden_in.shape
    pieces = PIECES if whole_rows % (16 * PIECES) == 0 else 1
    hidden_in = cut(hidden_in, 0, pieces)
    routes = cut(routes, 1, pieces)
    gate_probs = cut(gate_probs, 1, pieces)
    micro, rows, width = hidden_in.shape
    _, locals_, _, ff = w_gate.shape
    stages, zs, ys = (lax.axis_size(a) for a in ("pipe", "exp", "pair"))
    groups = zs * ys
    lanes = share_lanes(groups * locals_)
    dma = pltpu.SemaphoreType.DMA
    anywhere = pl.BlockSpec(memory_space=pl.ANY)
    inside = pl.BlockSpec(memory_space=pltpu.VMEM)
    out = pl.pallas_call(
        functools.partial(relay_kernel, stages, zs, ys, pieces),
        out_shape=jax.ShapeDtypeStruct((1, micro, rows, width), BF16),
        in_specs=[anywhere, inside, inside, inside, anywhere, anywhere, anywhere],
        out_specs=anywhere,
        scratch_shapes=[
            pltpu.VMEM((locals_, width, ff), BF16),
            pltpu.VMEM((locals_, width, ff), BF16),
            pltpu.VMEM((locals_ * ff, width), BF16),
            pltpu.VMEM((micro, rows, width), BF16),
            pltpu.VMEM((micro, groups * rows, width), BF16),
            pltpu.VMEM((groups, micro, rows, lanes), BF16),
            pltpu.VMEM((groups * rows, locals_ * ff), BF16),
            pltpu.VMEM((micro, groups * rows, width), BF16),
            pltpu.VMEM((micro, max(1, ys - 1), zs, rows, width), BF16),
            pltpu.VMEM((micro, zs, rows, width), BF16),
            pltpu.VMEM((micro, zs, rows, width), BF16),
            pltpu.VMEM((micro, rows, width), BF16),
            dma((3 * locals_,)),
            dma((micro,)),
            dma((micro,)),
            dma((micro,)),
            dma((groups,)),
            dma((groups,)),
            dma((micro, groups)),
            dma((micro, groups)),
            dma((micro, max(1, ys - 1), zs)),
            dma((micro, max(1, ys - 1), zs)),
            dma((micro, max(1, zs - 1))),
            dma((micro, zs)),
        ],
        compiler_params=pltpu.CompilerParams(
            collective_id=0, has_side_effects=True, vmem_limit_bytes=VMEM_LIMIT
        ),
    )(hidden_in, routes, gate_probs, norm_gain, w_gate, w_up, w_down)
    return out.reshape(1, batches, whole_rows, width)


def cut(value, axis, pieces):
    shape = value.shape
    rows = shape[axis + 1] // pieces
    return value.reshape(shape[:axis] + (shape[axis] * pieces, rows) + shape[axis + 2 :])


def share_lanes(experts):
    return -(-2 * experts // 128) * 128


def kernel_fits(hidden_in, w_gate, groups):
    micro, rows, width = hidden_in.shape
    _, locals_, _, ff = w_gate.shape
    weights = 3 * locals_ * width * ff
    moved = micro * rows * width * (4 * groups + 5)
    small = groups * rows * (locals_ * ff + micro * share_lanes(groups * locals_))
    fits = 2 * (weights + moved + small) + 8 * 1024 * 1024 < VMEM_LIMIT
    return fits and rows % 16 == 0 and width % 128 == 0 and ff % 128 == 0


def passed_along(value, axis, steps):
    count = lax.axis_size(axis)
    first, last = (max(0, -steps), min(count, count - steps))
    return lax.ppermute(value, axis, [(source, source + steps) for source in range(first, last)])


def expert_block(arrived, wgate, wupper, wdown):
    gate = jnp.einsum("nlcd,ldf->nlcf", arrived, wgate, preferred_element_type=jnp.float32)
    upward = jnp.einsum("nlcd,ldf->nlcf", arrived, wupper, preferred_element_type=jnp.float32)
    hidden = (jax.nn.silu(gate) * upward).astype(jnp.bfloat16)
    return jnp.einsum("nlcf,lfd->nlcd", hidden, wdown, preferred_element_type=jnp.float32).astype(
        jnp.bfloat16
    )


def on_device(hidden_in, routes, gate_probs, norm_gain, w_gate, w_up, w_down):
    if kernel_fits(hidden_in, w_gate, lax.axis_size(("exp", "pair"))):
        return relayed(hidden_in, routes, gate_probs, norm_gain, w_gate, w_up, w_down)
    section = lax.axis_index("pipe")
    micro, tok_rows, width = hidden_in.shape
    top_count = routes.shape[3]
    groups = lax.axis_size(("exp", "pair"))
    local_experts = w_gate.shape[1]
    experts = local_experts * groups
    capacity = max(2, 3 * tok_rows * top_count // (2 * experts))
    gain = norm_gain[0]
    wgate = w_gate[0]
    wupper = w_up[0]
    wdown = w_down[0]
    expert_ids = jnp.arange(experts, dtype=jnp.int32)

    def layer(state, index):
        chosen = lax.dynamic_index_in_dim(routes[0], index, 0, keepdims=False).reshape(-1)
        probs = lax.dynamic_index_in_dim(gate_probs[0], index, 0, keepdims=False)
        floated = state.astype(jnp.float32)
        scale = lax.rsqrt(jnp.mean(floated * floated, axis=-1, keepdims=True) + EPS)
        normed = (floated * scale * gain).astype(jnp.bfloat16)
        onehot = (chosen[:, None] == expert_ids[None, :]).astype(jnp.int32)
        before = jnp.cumsum(onehot, axis=0) - onehot
        slots = jnp.sum(before * onehot, axis=1)
        outgoing = jnp.zeros((experts, capacity, width), jnp.bfloat16)
        outgoing = outgoing.at[chosen, slots].set(jnp.repeat(normed, top_count, axis=0))
        grouped = outgoing.reshape(groups, local_experts, capacity, width)
        produced = expert_block(
            lax.all_to_all(grouped, ("exp", "pair"), split_axis=0, concat_axis=0, tiled=True),
            wgate,
            wupper,
            wdown,
        )
        returned = lax.all_to_all(
            produced, ("exp", "pair"), split_axis=0, concat_axis=0, tiled=True
        )
        results = returned.reshape(experts, capacity, width)[chosen, slots]
        results = results.reshape(tok_rows, top_count, width).astype(jnp.float32)
        weights = probs / jnp.sum(probs, axis=-1, keepdims=True)
        mixed = jnp.einsum("tk,tkd->td", weights, results)
        return (floated + mixed).astype(jnp.bfloat16)

    def advance(step, carry):
        received, saved = carry
        index = step - section
        valid = jnp.logical_and(index >= 0, index < micro)
        clipped = jnp.clip(index, 0, micro - 1)
        first = lax.dynamic_index_in_dim(hidden_in, clipped, 0, keepdims=False)
        state = jnp.where(section == 0, first, received)
        updated = layer(state, clipped)
        saved = jnp.where(valid, lax.dynamic_update_index_in_dim(saved, updated, clipped, 0), saved)
        received = passed_along(updated, "pipe", 1)
        return (received, saved)

    start = (
        jnp.zeros((tok_rows, width), jnp.bfloat16),
        jnp.zeros((micro, tok_rows, width), jnp.bfloat16),
    )
    received, saved = lax.fori_loop(0, micro + lax.axis_size("pipe") - 1, advance, start)
    return saved[None]


def solution(mesh):
    in_specs = (
        P(None, ("exp", "pair"), None),
        P("pipe", None, ("exp", "pair"), None),
        P("pipe", None, ("exp", "pair"), None),
        P("pipe", None),
        P("pipe", ("exp", "pair"), None, None),
        P("pipe", ("exp", "pair"), None, None),
        P("pipe", ("exp", "pair"), None, None),
    )
    out_specs = P("pipe", None, ("exp", "pair"), None)
    return jax.shard_map(
        on_device, mesh=mesh, in_specs=in_specs, out_specs=out_specs, check_vma=False
    )
```

profile of v0, /device:TPU:19, one launch (start us, length us, event | category | flops | bytes accessed | tf_op | source)
XLA Modules:
  0.0 219.2 jit_solution(3820292700102114826)
XLA Ops:
  0.0 1.4 copy.8
  1.4 1.4 copy.9
  2.8 214.4 %shard_map.73 = bf16[1,8,16,2048]{3,2,1,0:T(8,128)(2,1)} custom-call(bf16[8,16,2048]{2,1,0:T(8,128)(2,1)} %bitcast.5, s32[1,8,16,8]{3,2,1,0:T(8,128)} %bitcast.6, f32[1,8,16,8]{3,2,1,0:T(8,128)} %bitcast.7, f32[1,2048]{1,0:T(1,128)} %gain_ref.1, bf16[1,2,2048,768]{3,2,1,0:T(8,128)(2,1)} %wgate_ref.1, bf16[1,2,2048,768]{3,2,1,0:T(8,128)(2,1)} %wup_ref.1, ...), custom_call_target="tpu_custom_call" | custom-call | tf_op jit(solution)/shard_map/pallas_call | solution.py:403
  217.3 1.9 copy.11
where the time goes:
time: 220 us; the launch traced here: 219 us
  Pallas kernels  214 us (97%)
  local copies, waits for them, and re-layouts  4.73 us (2%)
    pallas_call x1, Pallas kernels, relayed(): pl.pallas_call(functools.partial(relay_kernel, stages, zs, ys, pieces), o...  214 us
    unnamed x3, local copies, waits for them, and re-layouts  4.73 us

commit v1 on v0

--- a/solution.py
+++ b/solution.py
@@ -12,6 +12,16 @@
 F32 = jnp.float32
 BF16 = jnp.bfloat16
 PIECES = 2
+AHEAD = 2
+RELAY_AHEAD = 2
+LOCAL = 1
+SPARE = 5
+SCHEDULE = (
+    (("C", 0, 0, 99), ("S", 0, 0, 99), ("E", 0, 0, 99), ("A", 0, 0, 99), ("F", 1, 0, 99)),
+    (("C", 0, 0, 99), ("S", 0, 0, 99), ("F", 1, 0, 99), ("E", 0, 0, 99)),
+    (("C", 0, 0, 99), ("F", 1, 0, 99), ("E", -1, 0, 99), ("S", 0, 0, 99)),
+    (("C", 0, 0, 99), ("F", 1, 0, 99), ("E", -1, 0, 99), ("S", 0, 0, 99)),
+)
 VMEM_LIMIT = 63 * 1024 * 1024
 
 
@@ -26,7 +36,6 @@
     stages,
     zs,
     ys,
-    pieces,
     hidden_ref,
     routes_ref,
     probs_ref,
@@ -41,12 +50,17 @@
     hbuf,
     tokens,
     share,
+    column,
     hid,
     part,
     fromy,
     zsend,
     fromz,
     obuf,
+    nbuf,
+    gnext,
+    relay,
+    gfirst,
     w_sem,
     h_sem,
     hs_sem,
@@ -55,14 +69,22 @@
     sr_sem,
     a_sem,
     ar_sem,
+    f_sem,
     y_sem,
     yr_sem,
     z_sem,
     zr_sem,
+    g_sem,
+    gr_sem,
+    hr_sem,
+    b_sem,
+    rr_sem,
+    q_sem,
+    v_sem,
 ):
     micro, rows, width = hbuf.shape
     locals_, _, ff = wg.shape
-    lanes = share.shape[3]
+    span = share.shape[2]
     groups = zs * ys
     experts = groups * locals_
     stage = lax.axis_index("pipe")
@@ -72,9 +94,21 @@
     slot = y * zs + z
     upper_half = lax.div(2 * z, zs)
     turn = 1 - 2 * upper_half
+    is_first = stage == 0
+    has_last = stage > 0
+    has_next = stage < stages - 1
+    helper = stages // 2
+    local = min(LOCAL, micro) if helper else micro
+    is_helper = jnp.logical_and(stage == helper, stage > 0)
+
+    def block(at):
+        return pl.ds(pl.multiple_of(at * rows, rows), rows)
 
     def along(k):
         return lax.rem(z + turn * k + zs, zs)
+
+    def across(dy):
+        return lax.rem(y + dy, ys)
 
     def peer(dz, dy):
         return lax.rem(z + dz, zs), lax.rem(y + dy, ys)
@@ -96,10 +130,19 @@
     def from_input(m):
         return pltpu.make_async_copy(hidden_ref.at[m], hbuf.at[m], h_sem.at[m])
 
-    @pl.when(stage == 0)
+    @pl.when(is_first)
     def _():
         for m in range(micro):
             from_input(m).start()
+
+    def relay_input(m):
+        here = relay.at[m, block(slot)]
+        return pltpu.make_async_copy(hidden_ref.at[m], here, hr_sem.at[m])
+
+    @pl.when(is_helper)
+    def _():
+        for m in range(local, micro):
+            relay_input(m).start()
 
     for j in range(locals_):
         loads[j][0].start()
@@ -112,30 +155,56 @@
         pz, py = peer(dz, dy)
         pl.semaphore_signal(barrier, inc=1, device_id={"exp": pz, "pair": py}, device_id_type=MESH)
 
-    @pl.when(stage > 0)
-    def _():
-        pl.semaphore_signal(barrier, inc=1, device_id={"pipe": stage - 1}, device_id_type=MESH)
-
-    @pl.when(stage < stages - 1)
-    def _():
-        pl.semaphore_signal(barrier, inc=1, device_id={"pipe": stage + 1}, device_id_type=MESH)
-
-    lane = lax.broadcasted_iota(jnp.int32, (rows, lanes), 1)
-    for m in range(micro):
+    @pl.when(has_last)
+    def _():
+        for k in range(zs):
+            pl.semaphore_signal(
+                barrier,
+                inc=1,
+                device_id={"pipe": stage - 1, "exp": along(k)},
+                device_id_type=MESH,
+            )
+
+    @pl.when(has_next)
+    def _():
+        for k in range(zs):
+            pl.semaphore_signal(
+                barrier,
+                inc=1,
+                device_id={"pipe": stage + 1, "exp": along(k)},
+                device_id_type=MESH,
+            )
+
+    if local < micro:
+
+        @pl.when(is_first)
+        def _():
+            pl.semaphore_signal(
+                barrier, inc=1, device_id={"pipe": helper}, device_id_type=MESH
+            )
+
+        @pl.when(is_helper)
+        def _():
+            pl.semaphore_signal(barrier, inc=1, device_id={"pipe": 0}, device_id_type=MESH)
+
+    batches, top, held_rows = routes_ref.shape[1:]
+    named_ids = lax.broadcasted_iota(jnp.int32, (experts, held_rows), 0)
+    for m in range(batches):
         probs = probs_ref[0, m]
-        normal = probs / jnp.sum(probs, axis=-1, keepdims=True)
+        normal = probs / jnp.sum(probs, axis=0, keepdims=True)
         chosen = routes_ref[0, m]
-        total = jnp.zeros((rows, lanes), F32)
-        for k in range(chosen.shape[1]):
-            named = chosen[:, k : k + 1]
-            hit = jnp.logical_or(lane == named, lane == named + experts)
-            total = total + jnp.where(hit, normal[:, k : k + 1], 0.0)
-        high = total.astype(BF16)
-        low = (total - high.astype(F32)).astype(BF16)
-        share[slot, m] = jnp.where(lane < experts, high, low)
-
-    linked = (stage > 0).astype(jnp.int32) + (stage < stages - 1).astype(jnp.int32)
-    pl.semaphore_wait(barrier, len(others) + linked)
+        total = jnp.zeros((experts, held_rows), F32)
+        for k in range(top):
+            total = total + jnp.where(
+                named_ids == chosen[k : k + 1], normal[k : k + 1], 0.0
+            )
+        share[slot, :, m * held_rows : (m + 1) * held_rows] = total
+
+    linked = has_last.astype(jnp.int32) + has_next.astype(jnp.int32)
+    awaited = len(others) + linked * zs
+    if local < micro:
+        awaited = awaited + is_first.astype(jnp.int32) + is_helper.astype(jnp.int32)
+    pl.semaphore_wait(barrier, awaited)
 
     def share_copy(at, to_z, to_y):
         return pltpu.make_async_remote_copy(
@@ -157,25 +226,97 @@
             pz, py = peer(dz, dy)
             share_copy(py * zs + pz, pz, py).wait_recv()
 
-    def token_copy(m, at, tag, to_z, to_y):
-        block = tokens.at[m, pl.ds(pl.multiple_of(at * rows, rows), rows)]
-        return pltpu.make_async_remote_copy(
-            src_ref=block,
-            dst_ref=block,
-            send_sem=a_sem.at[m, tag],
+    def gain_copy():
+        return pltpu.make_async_remote_copy(
+            src_ref=gain_ref,
+            dst_ref=gnext,
+            send_sem=g_sem.at[0],
+            recv_sem=gr_sem.at[0],
+            device_id={"pipe": stage - 1},
+            device_id_type=MESH,
+        )
+
+    def first_gain_copy():
+        return pltpu.make_async_remote_copy(
+            src_ref=gain_ref,
+            dst_ref=gfirst,
+            send_sem=g_sem.at[1],
+            recv_sem=gr_sem.at[1],
+            device_id={"pipe": helper},
+            device_id_type=MESH,
+        )
+
+    def relay_z(m, k):
+        here = relay.at[m, block(slot)]
+        return pltpu.make_async_remote_copy(
+            src_ref=here,
+            dst_ref=here,
+            send_sem=b_sem.at[m, k],
+            recv_sem=rr_sem.at[m, slot],
+            device_id={"exp": along(k)},
+            device_id_type=MESH,
+        )
+
+    def relay_y(m, at, dz, dy):
+        here = relay.at[m, block(at)]
+        return pltpu.make_async_remote_copy(
+            src_ref=here,
+            dst_ref=here,
+            send_sem=q_sem.at[m, dz * max(1, ys - 1) + dy - 1],
+            recv_sem=rr_sem.at[m, at],
+            device_id={"pair": across(dy)},
+            device_id_type=MESH,
+        )
+
+    def relay_x(m, at):
+        return pltpu.make_async_remote_copy(
+            src_ref=relay.at[m, block(at)],
+            dst_ref=tokens.at[m, block(at)],
+            send_sem=v_sem.at[m, at],
             recv_sem=ar_sem.at[m, at],
-            device_id={"exp": to_z, "pair": to_y},
+            device_id={"pipe": 0},
+            device_id_type=MESH,
+        )
+
+    def z_token(m, k):
+        here = tokens.at[m, block(slot)]
+        return pltpu.make_async_remote_copy(
+            src_ref=here,
+            dst_ref=here,
+            send_sem=a_sem.at[m, k],
+            recv_sem=ar_sem.at[m, slot],
+            device_id={"exp": along(k)},
+            device_id_type=MESH,
+        )
+
+    def next_token(m, k):
+        return pltpu.make_async_remote_copy(
+            src_ref=nbuf.at[m],
+            dst_ref=tokens.at[m, block(slot)],
+            send_sem=a_sem.at[m, k],
+            recv_sem=ar_sem.at[m, slot],
+            device_id={"pipe": stage + 1, "exp": along(k)},
+            device_id_type=MESH,
+        )
+
+    def y_token(m, at, dz, dy):
+        here = tokens.at[m, block(at)]
+        return pltpu.make_async_remote_copy(
+            src_ref=here,
+            dst_ref=here,
+            send_sem=f_sem.at[m, dz * max(1, ys - 1) + dy - 1],
+            recv_sem=ar_sem.at[m, at],
+            device_id={"pair": across(dy)},
             device_id_type=MESH,
         )
 
     def y_copy(m, dy, tz):
-        py = lax.rem(y + dy, ys)
-        return pltpu.make_async_remote_copy(
-            src_ref=part.at[m, pl.ds(pl.multiple_of((py * zs + tz) * rows, rows), rows)],
+        return pltpu.make_async_remote_copy(
+            src_ref=part.at[m, block(across(dy) * zs + tz)],
             dst_ref=fromy.at[m, dy - 1, tz],
             send_sem=y_sem.at[m, dy - 1, tz],
             recv_sem=yr_sem.at[m, dy - 1, tz],
-            device_id={"pair": py},
+            device_id={"pair": across(dy)},
             device_id_type=MESH,
         )
 
@@ -202,87 +343,117 @@
     def out_copy(m):
         return pltpu.make_async_copy(obuf.at[m], out_ref.at[0, m], o_sem.at[m])
 
+    def normed(state, gain):
+        scale = lax.rsqrt(jnp.mean(state * state, axis=-1, keepdims=True) + EPS)
+        return (state * scale * gain[...]).astype(BF16)
+
     def announce(m):
         from_input(m).wait()
-        state = hbuf[m].astype(F32)
-        scale = lax.rsqrt(jnp.mean(state * state, axis=-1, keepdims=True) + EPS)
-        tokens[m, pl.ds(pl.multiple_of(slot * rows, rows), rows)] = (
-            state * scale * gain_ref[...]
-        ).astype(BF16)
+        tokens[m, block(slot)] = normed(hbuf[m].astype(F32), gain_ref)
         for k in range(zs - 1, 0, -1):
-            token_copy(m, slot, k - 1, along(k), y).start()
+            z_token(m, k).start()
+
+    def relay_announce(m):
+        relay_input(m).wait()
+        relay[m, block(slot)] = normed(relay[m, block(slot)].astype(F32), gfirst)
+        for k in range(zs - 1, 0, -1):
+            relay_z(m, k).start()
+
+    def relay_near(m):
+        for dz in range(zs):
+            at = y * zs + along(dz)
+            if dz:
+                relay_y(m, at, dz, 0).wait_recv()
+            for dy in range(1, ys):
+                relay_y(m, at, dz, dy).start()
+            relay_x(m, at).start()
+
+    def relay_far(m):
         for dy in range(1, ys):
-            token_copy(m, slot, (zs - 1) + dy - 1, z, lax.rem(y + dy, ys)).start()
-
-    nz = zs - 1
-
-    def forward_tag(dz, dy):
-        return nz + (ys - 1) + (dz - 1) * (ys - 1) + dy - 1
-
-    def gather_z(m):
-        for dz in range(1, zs):
-            pz = along(dz)
-            at = y * zs + pz
-            token_copy(m, at, dz - 1, pz, y).wait_recv()
+            for dz in range(zs):
+                at = across(dy) * zs + along(dz)
+                relay_y(m, at, dz, dy).wait_recv()
+                relay_x(m, at).start()
+
+    def forward(m):
+        for dz in range(zs):
+            at = y * zs + along(dz)
+            if dz:
+                y_token(m, at, dz, 0).wait_recv()
+            else:
+
+                @pl.when(has_last)
+                def _():
+                    y_token(m, at, dz, 0).wait_recv()
+
             for dy in range(1, ys):
-                token_copy(m, at, forward_tag(dz, dy), z, lax.rem(y + dy, ys)).start()
-
-    def gather_y(m, dy):
-        py = lax.rem(y + dy, ys)
-        for dz in range(zs):
-            pz = lax.rem(z + dz, zs)
-            token_copy(m, py * zs + pz, 0, z, py).wait_recv()
+                y_token(m, at, dz, dy).start()
+
+    def arrive(m):
+        @pl.when(jnp.logical_and(is_first, m >= local))
+        def _():
+            for dz in range(zs):
+                relay_x(m, y * zs + along(dz)).wait_recv()
+
+        for dy in range(1, ys):
+            for dz in range(zs):
+                y_token(m, across(dy) * zs + along(dz), dz, dy).wait_recv()
 
     ftile = divisor_tile(ff, 256)
     ntile = divisor_tile(width, 512)
     count = groups * rows
 
-    def span(dy):
-        return 0, pl.ds(0, count)
-
-    def upper(m, dy):
-        at, block = span(dy)
-        wide = lax.broadcasted_iota(jnp.int32, (count, lanes), 1)
-        shares = share[:, m].reshape(count, lanes).astype(F32)
+    def spread():
+        ids = lax.broadcasted_iota(jnp.int32, (groups, experts, span), 1)
+        held = share[...]
+        mine = [
+            jnp.sum(jnp.where(ids == me * locals_ + j, held, 0.0), axis=1)
+            for j in range(locals_)
+        ]
+        padding = jnp.zeros((128 - locals_ * groups, span), F32)
+        column[...] = jnp.transpose(jnp.concatenate(mine + [padding], axis=0))
+
+    def upper(m):
+        weights = column[pl.ds(pl.multiple_of(m * rows, rows), rows)]
         for j in range(locals_):
-            expert = me * locals_ + j
-            mine = jnp.logical_or(wide == expert, wide == expert + experts)
-            column = jnp.sum(jnp.where(mine, shares, 0.0), axis=-1, keepdims=True)
-            if dy == 0:
-
-                @pl.when(m == 0)
-                def _():
-                    loads[j][0].wait()
-                    loads[j][1].wait()
+            scaled = jnp.concatenate(
+                [weights[:, j * groups + g : j * groups + g + 1] for g in range(groups)], axis=0
+            )
+
+            @pl.when(m == 0)
+            def _():
+                loads[j][0].wait()
+                loads[j][1].wait()
 
             for c in range(0, ff, ftile):
-                held = tokens[m, block]
+                held = tokens[m]
                 gate = jnp.dot(held, wg[j, :, c : c + ftile], preferred_element_type=F32)
                 upward = jnp.dot(held, wu[j, :, c : c + ftile], preferred_element_type=F32)
-                hid[block, j * ff + c : j * ff + c + ftile] = (
-                    jax.nn.silu(gate) * upward * column
+                hid[:, j * ff + c : j * ff + c + ftile] = (
+                    jax.nn.silu(gate) * upward * scaled
                 ).astype(BF16)
 
-    def lower(m, dy):
-        _, block = span(dy)
-        for c in range(0, width, ntile):
-            part[m, block, c : c + ntile] = jnp.dot(
-                hid[block], wd[:, c : c + ntile], preferred_element_type=F32
-            ).astype(BF16)
-
-    def down_wait(m):
+    def lower(m):
         @pl.when(m == 0)
         def _():
             for j in range(locals_):
                 loads[j][2].wait()
 
+        for c in range(0, width, ntile):
+            part[m, :, c : c + ntile] = jnp.dot(
+                hid[...], wd[:, c : c + ntile], preferred_element_type=F32
+            ).astype(BF16)
+
+    def compute(m):
+        arrive(m)
+        upper(m)
+        lower(m)
+        for dy in range(1, ys):
+            for k in range(zs - 1, -1, -1):
+                y_copy(m, dy, along(k)).start()
+
     def own_part(m, pz):
-        at = pl.multiple_of((y * zs + pz) * rows, rows)
-        return part[m, pl.ds(at, rows)].astype(F32)
-
-    def send_y(m, dy):
-        for k in range(zs - 1, -1, -1):
-            y_copy(m, dy, along(k)).start()
+        return part[m, block(y * zs + pz)].astype(F32)
 
     def scatter(m):
         for k in range(zs - 1, 0, -1):
@@ -295,6 +466,10 @@
             z_copy(m, k, z).start()
 
     def finish(m):
+        @pl.when(jnp.logical_or(has_last, m >= local))
+        def _():
+            from_input(m).wait()
+
         total = hbuf[m].astype(F32) + own_part(m, z)
         for dy in range(1, ys):
             y_copy(m, dy, z).wait_recv()
@@ -302,86 +477,145 @@
         for k in range(1, zs):
             z_copy(m, k, along(k)).wait_recv()
             total = total + fromz[m, along(k)].astype(F32)
-        obuf[m] = total.astype(BF16)
-
-        @pl.when(stage < stages - 1)
-        def _():
+        state = total.astype(BF16)
+        obuf[m] = state
+
+        @pl.when(has_next)
+        def _():
+            nbuf[m] = normed(state.astype(F32), gnext)
+            for k in range(zs - 1, -1, -1):
+                next_token(m, k).start()
             hand_copy(m).start()
 
         out_copy(m).start()
 
-    for i in range(pieces):
-        announce(i)
+    @pl.when(is_first)
+    def _():
+        if local < micro:
+            first_gain_copy().start()
+        for m in range(min(AHEAD, local)):
+            announce(m)
+
+    @pl.when(has_last)
+    def _():
+        gain_copy().start()
+
     share_send()
 
-    @pl.when(stage == 0)
-    def _():
-        for i in range(pieces):
-            gather_z(i)
-
-    @pl.loop(0, micro // pieces)
-    def _(batch):
-        m = batch * pieces
-        following = m + pieces < micro
-        first = jnp.logical_and(stage == 0, following)
-        later = jnp.logical_and(stage > 0, following)
-
-        @pl.when(stage > 0)
-        def _():
-            for i in range(pieces):
-                gather_z(m + i)
-
-        @pl.when(first)
-        def _():
-            for i in range(pieces):
-                announce(m + pieces + i)
-
-        @pl.when(m == 0)
-        def _():
-            share_wait()
-
-        for i in range(pieces):
-            for dy in range(1, ys):
-                gather_y(m + i, dy)
-            upper(m + i, 0)
-            if i == 0:
-                down_wait(m)
-            lower(m + i, 0)
-            for dy in range(1, ys):
-                send_y(m + i, dy)
-
-        @pl.when(first)
-        def _():
-            for i in range(pieces):
-                gather_z(m + pieces + i)
-
-        for i in range(pieces):
-            scatter(m + i)
-        for i in range(pieces):
-            finish(m + i)
-
-        @pl.when(later)
-        def _():
-            for i in range(pieces):
-                announce(m + pieces + i)
+    @pl.when(is_helper)
+    def _():
+        if local < micro:
+            first_gain_copy().wait_recv()
+            for m in range(local, min(micro, local + RELAY_AHEAD)):
+                relay_announce(m)
+
+            @pl.loop(local, micro + 1)
+            def _(m):
+                @pl.when(m < micro)
+                def _():
+                    relay_near(m)
+
+                @pl.when(m + RELAY_AHEAD < micro)
+                def _():
+                    relay_announce(m + RELAY_AHEAD)
+
+                @pl.when(m > local)
+                def _():
+                    relay_far(m - 1)
+
+    @pl.when(has_next)
+    def _():
+        gain_copy().wait_recv()
+
+    share_wait()
+    spread()
+    handlers = {"A": announce, "F": forward, "S": scatter, "E": finish}
+    centre = [[item[0] for item in listed].index("C") for listed in SCHEDULE]
+
+    def serve(step, late):
+        for at, listed in enumerate(SCHEDULE[:stages]):
+            items = listed[centre[at] + 1 :] if late else listed[: centre[at]]
+            mine = stage == at if at + 1 < len(SCHEDULE) else stage >= at
+
+            @pl.when(mine)
+            def _():
+                for name, lead, low, high in items:
+                    m = step + lead
+                    if name in "AF" and at == 0:
+                        high = min(high, local)
+                    if name == "A":
+                        low = max(low, AHEAD)
+                    if low >= min(high, micro):
+                        continue
+
+                    @pl.when(jnp.logical_and(m >= low, m < min(high, micro)))
+                    def _():
+                        handlers[name](m)
+
+    @pl.loop(0, micro + SPARE)
+    def _(turn_number):
+        step = turn_number - 1
+        serve(step, False)
+
+        @pl.when(jnp.logical_and(step >= 0, step < micro))
+        def _():
+            compute(step)
+
+        serve(step, True)
 
     for dz, dy in others:
         pz, py = peer(dz, dy)
         share_copy(slot, pz, py).wait_send()
 
+    @pl.when(has_last)
+    def _():
+        gain_copy().wait_send()
+
+    if local < micro:
+
+        @pl.when(is_first)
+        def _():
+            first_gain_copy().wait_send()
+
+        @pl.when(is_helper)
+        def _():
+            @pl.loop(local, micro)
+            def _(m):
+                for k in range(1, zs):
+                    relay_z(m, k).wait_send()
+                for dz in range(zs):
+                    for dy in range(1, ys):
+                        relay_y(m, slot, dz, dy).wait_send()
+                for at in range(groups):
+                    relay_x(m, at).wait_send()
+
     @pl.loop(0, micro)
     def _(m):
-        for tag in range(groups - 1):
-            token_copy(m, slot, tag, z, y).wait_send()
+        for k in range(1, zs):
+            z_copy(m, k, z).wait_send()
+
+        direct = jnp.logical_or(has_last, m < local)
+
+        @pl.when(jnp.logical_and(is_first, direct))
+        def _():
+            for k in range(1, zs):
+                z_token(m, k).wait_send()
+
+        @pl.when(direct)
+        def _():
+            for dy in range(1, ys):
+                for tz in range(zs):
+                    y_token(m, slot, tz, dy).wait_send()
+
+        @pl.when(has_next)
+        def _():
+            for k in range(zs):
+                next_token(m, k).wait_send()
+            hand_copy(m).wait_send()
+
         for dy in range(1, ys):
             for tz in range(zs):
                 y_copy(m, dy, tz).wait_send()
-        for dz in range(1, zs):
-            z_copy(m, dz, z).wait_send()
-
-        @pl.when(stage < stages - 1)
-        def _():
-            hand_copy(m).wait_send()
 
         out_copy(m).wait()
 
@@ -390,18 +624,17 @@
     batches, whole_rows, _ = hidden_in.shape
     pieces = PIECES if whole_rows % (16 * PIECES) == 0 else 1
     hidden_in = cut(hidden_in, 0, pieces)
-    routes = cut(routes, 1, pieces)
-    gate_probs = cut(gate_probs, 1, pieces)
+    routes = jnp.transpose(routes, (0, 1, 3, 2))
+    gate_probs = jnp.transpose(gate_probs, (0, 1, 3, 2))
     micro, rows, width = hidden_in.shape
     _, locals_, _, ff = w_gate.shape
     stages, zs, ys = (lax.axis_size(a) for a in ("pipe", "exp", "pair"))
     groups = zs * ys
-    lanes = share_lanes(groups * locals_)
     dma = pltpu.SemaphoreType.DMA
     anywhere = pl.BlockSpec(memory_space=pl.ANY)
     inside = pl.BlockSpec(memory_space=pltpu.VMEM)
     out = pl.pallas_call(
-        functools.partial(relay_kernel, stages, zs, ys, pieces),
+        functools.partial(relay_kernel, stages, zs, ys),
         out_shape=jax.ShapeDtypeStruct((1, micro, rows, width), BF16),
         in_specs=[anywhere, inside, inside, inside, anywhere, anywhere, anywhere],
         out_specs=anywhere,
@@ -411,25 +644,38 @@
             pltpu.VMEM((locals_ * ff, width), BF16),
             pltpu.VMEM((micro, rows, width), BF16),
             pltpu.VMEM((micro, groups * rows, width), BF16),
-            pltpu.VMEM((groups, micro, rows, lanes), BF16),
+            pltpu.VMEM((groups, groups * locals_, micro * rows), F32),
+            pltpu.VMEM((micro * rows, 128), F32),
             pltpu.VMEM((groups * rows, locals_ * ff), BF16),
             pltpu.VMEM((micro, groups * rows, width), BF16),
             pltpu.VMEM((micro, max(1, ys - 1), zs, rows, width), BF16),
             pltpu.VMEM((micro, zs, rows, width), BF16),
             pltpu.VMEM((micro, zs, rows, width), BF16),
             pltpu.VMEM((micro, rows, width), BF16),
+            pltpu.VMEM((micro, rows, width), BF16),
+            pltpu.VMEM((1, width), F32),
+            pltpu.VMEM((micro, groups * rows, width), BF16),
+            pltpu.VMEM((1, width), F32),
             dma((3 * locals_,)),
             dma((micro,)),
             dma((micro,)),
             dma((micro,)),
             dma((groups,)),
             dma((groups,)),
+            dma((micro, zs)),
             dma((micro, groups)),
-            dma((micro, groups)),
+            dma((micro, zs * max(1, ys - 1))),
             dma((micro, max(1, ys - 1), zs)),
             dma((micro, max(1, ys - 1), zs)),
             dma((micro, max(1, zs - 1))),
             dma((micro, zs)),
+            dma((2,)),
+            dma((2,)),
+            dma((micro,)),
+            dma((micro, zs)),
+            dma((micro, groups)),
+            dma((micro, zs * max(1, ys - 1))),
+            dma((micro, groups)),
         ],
         compiler_params=pltpu.CompilerParams(
             collective_id=0, has_side_effects=True, vmem_limit_bytes=VMEM_LIMIT
@@ -444,18 +690,15 @@
     return value.reshape(shape[:axis] + (shape[axis] * pieces, rows) + shape[axis + 2 :])
 
 
-def share_lanes(experts):
-    return -(-2 * experts // 128) * 128
-
-
 def kernel_fits(hidden_in, w_gate, groups):
     micro, rows, width = hidden_in.shape
     _, locals_, _, ff = w_gate.shape
     weights = 3 * locals_ * width * ff
-    moved = micro * rows * width * (4 * groups + 5)
-    small = groups * rows * (locals_ * ff + micro * share_lanes(groups * locals_))
+    moved = micro * rows * width * (5 * groups + 6)
+    small = groups * rows * (locals_ * ff + 2 * micro * groups * locals_)
     fits = 2 * (weights + moved + small) + 8 * 1024 * 1024 < VMEM_LIMIT
-    return fits and rows % 16 == 0 and width % 128 == 0 and ff % 128 == 0
+    small_enough = groups * locals_ <= 128 and micro * rows % 128 == 0
+    return fits and small_enough and rows % 16 == 0 and width % 128 == 0 and ff % 128 == 0
 
 
 def passed_along(value, axis, steps):

time: 220 us -> 205 us (0.932)
  Pallas kernels: 214 us -> 202 us
  local copies, waits for them, and re-layouts: 4.73 us -> 1.88 us
    pallas_call x1, Pallas kernels: 214 us -> 202 us  [relayed(): pl.pallas_call(functools.partial(relay_kernel, stages, zs, ys), out_shape...]
    unnamed x3 -> x1, local copies, waits for them, and re-layouts: 4.73 us -> 1.88 us
where the time goes in v1:
time: 205 us; the launch traced here: 204 us
  Pallas kernels  202 us (99%)
    pallas_call x1, Pallas kernels, relayed(): pl.pallas_call(functools.partial(relay_kernel, stages, zs, ys), out_shape...  202 us

profile of v1, /device:TPU:19, one launch (start us, length us, event | category | flops | bytes accessed | tf_op | source)
XLA Modules:
  0.0 203.9 jit_solution(9533542777437853807)
XLA Ops:
  0.0 202.0 %shard_map.73 = bf16[1,8,16,2048]{3,2,1,0:T(8,128)(2,1)} custom-call(bf16[8,16,2048]{2,1,0:T(8,128)(2,1)} %bitcast.5, s32[1,4,8,32]{3,2,1,0:T(8,128)} %bitcast.6, f32[1,4,8,32]{3,2,1,0:T(8,128)} %bitcast.7, f32[1,2048]{1,0:T(1,128)} %gain_ref.1, bf16[1,2,2048,768]{3,2,1,0:T(8,128)(2,1)} %wgate_ref.1, bf16[1,2,2048,768]{3,2,1,0:T(8,128)(2,1)} %wup_ref.1, ...), custom_call_target="tpu_custom_call" | custom-call | tf_op jit(solution)/shard_map/pallas_call | solution.py:636
  202.0 1.9 copy.9

commit v2 on v1

--- a/solution.py
+++ b/solution.py
@@ -12,15 +12,13 @@
 F32 = jnp.float32
 BF16 = jnp.bfloat16
 PIECES = 2
-AHEAD = 2
 RELAY_AHEAD = 2
-LOCAL = 1
-SPARE = 5
+LOCAL = 2
 SCHEDULE = (
-    (("C", 0, 0, 99), ("S", 0, 0, 99), ("E", 0, 0, 99), ("A", 0, 0, 99), ("F", 1, 0, 99)),
-    (("C", 0, 0, 99), ("S", 0, 0, 99), ("F", 1, 0, 99), ("E", 0, 0, 99)),
-    (("C", 0, 0, 99), ("F", 1, 0, 99), ("E", -1, 0, 99), ("S", 0, 0, 99)),
-    (("C", 0, 0, 99), ("F", 1, 0, 99), ("E", -1, 0, 99), ("S", 0, 0, 99)),
+    ("FF", "", "S", "SE", "E", "SSS", "EEE", "S", "SEESE"),
+    ("FF", "", "SFEFS", "ES", "EFS", "ESFEF", "S", "EFSE", "SE"),
+    ("F", "FS", "ESFFE", "", "FSSFE", "", "FSEEF", "S", "SESEE"),
+    ("F", "SF", "SF", "FESFE", "FE", "F", "SFS", "SEE", "SSEEE"),
 )
 VMEM_LIMIT = 63 * 1024 * 1024
 
@@ -30,6 +28,46 @@
     while size % tile:
         tile //= 2
     return tile
+
+
+def merged(one, two):
+    best = {(len(one), len(two)): ""}
+    for i in range(len(one), -1, -1):
+        for j in range(len(two), -1, -1):
+            options = []
+            if i < len(one) and j < len(two) and one[i] == two[j]:
+                options.append(one[i] + best[i + 1, j + 1])
+            if i < len(one):
+                options.append(one[i] + best[i + 1, j])
+            if j < len(two):
+                options.append(two[j] + best[i, j + 1])
+            if options:
+                best[i, j] = min(options, key=len)
+    return best[0, 0]
+
+
+def plan_of(stages, micro, local):
+    tuned = len(SCHEDULE) == stages and len(SCHEDULE[0]) == micro + 1 and local == LOCAL
+    plans = []
+    for at in range(stages):
+        if tuned:
+            gaps = SCHEDULE[at]
+        elif at == 0:
+            gaps = ("F" * local,) + ("SE",) * micro
+        else:
+            gaps = ("F",) + ("SFE",) * (micro - 1) + ("SE",)
+        slots = functools.reduce(merged, gaps)
+        tables = [[] for _ in slots]
+        counts = {}
+        for step, gap in enumerate(gaps):
+            place = 0
+            for name in gap:
+                place = slots.index(name, place)
+                tables[place].append((step, counts.get(name, 0)))
+                counts[name] = counts.get(name, 0) + 1
+                place += 1
+        plans.append(list(zip(slots, tables)))
+    return plans
 
 
 def relay_kernel(
@@ -493,7 +531,7 @@
     def _():
         if local < micro:
             first_gain_copy().start()
-        for m in range(min(AHEAD, local)):
+        for m in range(local):
             announce(m)
 
     @pl.when(has_last)
@@ -529,39 +567,27 @@
 
     share_wait()
     spread()
-    handlers = {"A": announce, "F": forward, "S": scatter, "E": finish}
-    centre = [[item[0] for item in listed].index("C") for listed in SCHEDULE]
-
-    def serve(step, late):
-        for at, listed in enumerate(SCHEDULE[:stages]):
-            items = listed[centre[at] + 1 :] if late else listed[: centre[at]]
-            mine = stage == at if at + 1 < len(SCHEDULE) else stage >= at
-
-            @pl.when(mine)
+    handlers = {"F": forward, "S": scatter, "E": finish}
+    plans = plan_of(stages, micro, local)
+
+    @pl.loop(0, micro + 1)
+    def _(step):
+        for at, plan in enumerate(plans):
+
+            @pl.when(stage == at)
             def _():
-                for name, lead, low, high in items:
-                    m = step + lead
-                    if name in "AF" and at == 0:
-                        high = min(high, local)
-                    if name == "A":
-                        low = max(low, AHEAD)
-                    if low >= min(high, micro):
-                        continue
-
-                    @pl.when(jnp.logical_and(m >= low, m < min(high, micro)))
+                for name, table in plan:
+                    m = jnp.int32(-1)
+                    for when, piece in table:
+                        m = jnp.where(step == when, piece, m)
+
+                    @pl.when(m >= 0)
                     def _():
                         handlers[name](m)
 
-    @pl.loop(0, micro + SPARE)
-    def _(turn_number):
-        step = turn_number - 1
-        serve(step, False)
-
-        @pl.when(jnp.logical_and(step >= 0, step < micro))
+        @pl.when(step < micro)
         def _():
             compute(step)
-
-        serve(step, True)
 
     for dz, dy in others:
         pz, py = peer(dz, dy)

time: 205 us -> 192 us (0.937)
  Pallas kernels: 202 us -> 189 us
    pallas_call x1, Pallas kernels: 202 us -> 189 us  [relayed(): pl.pallas_call(functools.partial(relay_kernel, stages, zs, ys), out_shape...]
where the time goes in v2:
time: 192 us; the launch traced here: 191 us
  Pallas kernels  189 us (98%)
    pallas_call x1, Pallas kernels, relayed(): pl.pallas_call(functools.partial(relay_kernel, stages, zs, ys), out_shape...  189 us

profile of v2, /device:TPU:19, one launch (start us, length us, event | category | flops | bytes accessed | tf_op | source)
XLA Modules:
  0.0 190.8 jit_solution(5547221252504189879)
XLA Ops:
  0.0 188.9 %shard_map.73 = bf16[1,8,16,2048]{3,2,1,0:T(8,128)(2,1)} custom-call(bf16[8,16,2048]{2,1,0:T(8,128)(2,1)} %bitcast.5, s32[1,4,8,32]{3,2,1,0:T(8,128)} %bitcast.6, f32[1,4,8,32]{3,2,1,0:T(8,128)} %bitcast.7, f32[1,2048]{1,0:T(1,128)} %gain_ref.1, bf16[1,2,2048,768]{3,2,1,0:T(8,128)(2,1)} %wgate_ref.1, bf16[1,2,2048,768]{3,2,1,0:T(8,128)(2,1)} %wup_ref.1, ...), custom_call_target="tpu_custom_call" | custom-call | tf_op jit(solution)/shard_map/pallas_call | solution.py:662
  188.9 1.9 copy.9

commit v3 on v2

--- a/solution.py
+++ b/solution.py
@@ -15,7 +15,7 @@
 RELAY_AHEAD = 2
 LOCAL = 2
 SCHEDULE = (
-    ("FF", "", "S", "SE", "E", "SSS", "EEE", "S", "SEESE"),
+    ("FF", "", "S", "SE", "SE", "SE", "SE", "SE", "SESEE"),
     ("FF", "", "SFEFS", "ES", "EFS", "ESFEF", "S", "EFSE", "SE"),
     ("F", "FS", "ESFFE", "", "FSSFE", "", "FSEEF", "S", "SESEE"),
     ("F", "SF", "SF", "FESFE", "FE", "F", "SFS", "SEE", "SSEEE"),

time: 192 us -> 190 us (0.990)
  no operation moved by 1% of the time
where the time goes in v3:
time: 190 us
  Pallas kernels  188 us (99%)
    pallas_call x1, Pallas kernels, relayed(): pl.pallas_call(functools.partial(relay_kernel, stages, zs, ys), out_shape...  188 us

profile of v3, /device:TPU:19, one launch (start us, length us, event | category | flops | bytes accessed | tf_op | source)
XLA Modules:
  0.0 189.9 jit_solution(18068870581733481197)
XLA Ops:
  0.0 188.0 %shard_map.73 = bf16[1,8,16,2048]{3,2,1,0:T(8,128)(2,1)} custom-call(bf16[8,16,2048]{2,1,0:T(8,128)(2,1)} %bitcast.5, s32[1,4,8,32]{3,2,1,0:T(8,128)} %bitcast.6, f32[1,4,8,32]{3,2,1,0:T(8,128)} %bitcast.7, f32[1,2048]{1,0:T(1,128)} %gain_ref.1, bf16[1,2,2048,768]{3,2,1,0:T(8,128)(2,1)} %wgate_ref.1, bf16[1,2,2048,768]{3,2,1,0:T(8,128)(2,1)} %wup_ref.1, ...), custom_call_target="tpu_custom_call" | custom-call | tf_op jit(solution)/shard_map/pallas_call | solution.py:662
  188.0 1.9 copy.9
